TPU v7x, 256 devices: a whole 4x4x8 slice. The times are simulated.
256 devices in a mesh: replica: 64 (over z, y, core), model: 4 (over x).
Axes of the slice: x: 4, y: 4, z: 8, core: 2. Of those that a mesh axis runs over, the one named last changes fastest.
Arguments:
- partial_up: float32 [64, 1024, 4096], P('replica', None, 'model'), may hold values from -8 to 8
- partial_down: float32 [64, 4096, 1024], P('replica', 'model'), may hold values from -8 to 8
- partial_norm: float32 [64, 1024], P('replica'), may hold values from -16 to 16
- partial_bias: float32 [64, 1024], P('replica'), may hold values from -16 to 16
- master_up: float32 [1024, 4096], P('replica', 'model'), may hold values from -0.1875 to 0.1875
- master_down: float32 [4096, 1024], P('model', 'replica'), may hold values from -0.09375 to 0.09375
- master_norm: float32 [1024], P('replica'), may hold values from 0.25 to 1.75
- master_bias: float32 [1024], P('replica'), may hold values from -3 to 3
- memory_up: float32 [1024, 4096], P('replica', 'model'), may hold values from 0.05 to 0.8
- memory_down: float32 [4096, 1024], P('model', 'replica'), may hold values from 0.05 to 0.8
- memory_norm: float32 [1024], P('replica'), may hold values from 0.05 to 0.8
- memory_bias: float32 [1024], P('replica'), may hold values from 0.05 to 0.8
Outputs:
- compute_up: bfloat16 [1024, 4096], P(None, 'model')
- compute_down: bfloat16 [4096, 1024], P('model')
- compute_norm: bfloat16 [1024], replicated
- compute_bias: bfloat16 [1024], replicated
- stepped_up: float32 [1024, 4096], P('replica', 'model')
- stepped_down: float32 [4096, 1024], P('model', 'replica')
- stepped_norm: float32 [1024], P('replica')
- stepped_bias: float32 [1024], P('replica')
- state_new_up: float32 [1024, 4096], P('replica', 'model')
- state_new_down: float32 [4096, 1024], P('model', 'replica')
- state_new_norm: float32 [1024], P('replica')
- state_new_bias: float32 [1024], P('replica')
All inputs are finite; a program needn't handle non-finite values.
Results may differ from a plain program's by a relative error of at most 0.001.
Values may be sent and summed in bfloat16 or wider, within the bound.
A program may use at most 128 MiB of HBM per device.

v0:
```python
import jax
import jax.numpy as jnp
from jax import lax
from jax.sharding import PartitionSpec as P

learn_rate = 0.05
hold_rate = 0.9


def in_blocks(shard, dim, size):
    before, after = (shard.shape[:dim], shard.shape[dim + 1 :])
    return jnp.moveaxis(shard.reshape(*before, size, -1, *after), dim, 0)


def sum_packed(arrays, axis, dims):
    size = lax.axis_size(axis)
    tiles = [in_blocks(a, dim, size) for a, dim in zip(arrays, dims)]
    lines = jnp.concatenate([b.reshape(size, -1) for b in tiles], axis=1)
    width = max(16, -(-lines.shape[1] // 1024) * 8)
    lines = jnp.pad(lines, ((0, 0), (0, width * 128 - lines.shape[1]))).reshape(-1, 128)
    line, at, done = (lax.psum_scatter(lines, axis, tiled=True).reshape(-1), 0, [])
    for b in tiles:
        part = b[0]
        done.append(line[at : at + part.size].reshape(part.shape))
        at += part.size
    return tuple(done)


def from_everyone(shard, axis):
    size = lax.axis_size(axis)
    return lax.all_to_all(
        jnp.broadcast_to(shard[None], (size, *shard.shape)), axis, 0, 0, tiled=True
    )


def over_copies(shard, axis):
    everything = from_everyone(shard, axis)
    return jnp.sum(everything, axis=0)


def packed_total(arrays, axis):
    ends = [0]
    for a in arrays:
        ends.append(ends[-1] + a.size)
    total = over_copies(jnp.concatenate([a.ravel() for a in arrays]), axis)
    return tuple((total[b:e].reshape(a.shape) for a, b, e in zip(arrays, ends, ends[1:])))


def gather_turned(arrays, axis, dims):
    turned = [jnp.moveaxis(a, dim, 0) for a, dim in zip(arrays, dims)]
    both = jnp.concatenate([t.reshape(len(t), -1) for t in turned], axis=1)
    out, at, done = (lax.all_gather(both, axis, axis=0, tiled=True), 0, [])
    for t, dim in zip(turned, dims):
        section = out[:, at : at + t[0].size].reshape(-1, *t.shape[1:])
        done.append(jnp.moveaxis(section, 0, dim))
        at += t[0].size
    return tuple(done)


def on_device(
    partial_up,
    partial_down,
    partial_norm,
    partial_bias,
    master_up,
    master_down,
    master_norm,
    master_bias,
    memory_up,
    memory_down,
    memory_norm,
    memory_bias,
):
    mean_up, mean_down = sum_packed((partial_up[0], partial_down[0]), "replica", (0, 1))
    whole_norm, whole_bias = packed_total((partial_norm[0], partial_bias[0]), "replica")
    place = lax.axis_index("replica")
    mean_norm = lax.dynamic_slice_in_dim(
        whole_norm, place * master_norm.shape[0], master_norm.shape[0]
    )
    mean_bias = lax.dynamic_slice_in_dim(
        whole_bias, place * master_bias.shape[0], master_bias.shape[0]
    )
    mean_rate = lax.axis_size("replica") ** (-0.5)
    mean_up = mean_up * mean_rate
    mean_down = mean_down * mean_rate
    mean_norm = mean_norm * mean_rate
    mean_bias = mean_bias * mean_rate
    state_new_up = hold_rate * memory_up + (1.0 - hold_rate) * mean_up * mean_up
    stepped_up = master_up - learn_rate * mean_up * lax.rsqrt(state_new_up + 1e-06)
    state_new_down = hold_rate * memory_down + (1.0 - hold_rate) * mean_down * mean_down
    stepped_down = master_down - learn_rate * mean_down * lax.rsqrt(state_new_down + 1e-06)
    state_new_norm = hold_rate * memory_norm + (1.0 - hold_rate) * mean_norm * mean_norm
    stepped_norm = master_norm - learn_rate * mean_norm * lax.rsqrt(state_new_norm + 1e-06)
    state_new_bias = hold_rate * memory_bias + (1.0 - hold_rate) * mean_bias * mean_bias
    stepped_bias = master_bias - learn_rate * mean_bias * lax.rsqrt(state_new_bias + 1e-06)
    compute_up, compute_down, compute_norm, compute_bias = gather_turned(
        (
            stepped_up.astype(jnp.bfloat16),
            stepped_down.astype(jnp.bfloat16),
            stepped_norm.astype(jnp.bfloat16),
            stepped_bias.astype(jnp.bfloat16),
        ),
        "replica",
        (0, 1, 0, 0),
    )
    return (
        compute_up,
        compute_down,
        compute_norm,
        compute_bias,
        stepped_up,
        stepped_down,
        stepped_norm,
        stepped_bias,
        state_new_up,
        state_new_down,
        state_new_norm,
        state_new_bias,
    )


def solution(mesh):
    in_specs = (
        P("replica", None, "model"),
        P("replica", "model", None),
        P("replica", None),
        P("replica", None),
        P("replica", "model"),
        P("model", "replica"),
        P("replica"),
        P("replica"),
        P("replica", "model"),
        P("model", "replica"),
        P("replica"),
        P("replica"),
    )
    out_specs = (
        P(None, "model"),
        P("model", None),
        P(),
        P(),
        P("replica", "model"),
        P("model", "replica"),
        P("replica"),
        P("replica"),
        P("replica", "model"),
        P("model", "replica"),
        P("replica"),
        P("replica"),
    )
    return jax.shard_map(
        on_device, mesh=mesh, in_specs=in_specs, out_specs=out_specs, check_vma=False
    )
```

profile of v0, /device:TPU:1, one launch (start us, length us, event | category | flops | bytes accessed | tf_op | source)
XLA Modules:
  0.0 303.0 jit_solution(8466722291256023141)
XLA Ops:
  7.2 0.0 reduce-scatter.2.cloned.1.call-start
  7.2 5.4 %copy.56 = f32[1,1024,1024]{1,2,0:T(8,128)} copy(f32[1,1024,1024]{2,1,0:T(8,128)} %param.13) | data formatting | bytes 8388608 | tf_op args[1]
  12.6 8.7 %copy.57 = f32[64,1024,16]{0,2,1:T(8,128)} copy(f32[64,1024,16]{1,2,0:T(8,128)} %bitcast.15) | data formatting | bytes 8388608 | tf_op jit(solution)/shard_map/transpose | solution.py:12
  21.3 6.8 %copy.58 = f32[64,16384]{1,0:T(8,128)} copy(f32[64,16384]{0,1:T(8,128)} %bitcast.14) | data formatting | bytes 8388608 | tf_op jit(solution)/shard_map/reshape | solution.py:18
  28.1 4.9 %reshape_reshape_squeeze.3 = f32[64,16384]{1,0:T(8,128)} reshape(f32[1,1024,1024]{2,1,0:T(8,128)} %param.12) | data formatting | bytes 8388608 | tf_op jit(solution)/shard_map/reshape;reshape;squeeze | solution.py:18
  33.0 7.3 %pad_maximum_fusion = f32[64,32768]{1,0:T(8,128)} fusion(f32[64,16384]{1,0:T(8,128)} %copy.58, f32[64,16384]{1,0:T(8,128)} %reshape_reshape_squeeze.3), kind=kLoop, calls=%fused_computation | loop fusion | flops 2097152 | bytes 16777216 | tf_op jit(solution)/shard_map/concatenate | solution.py:18
  40.3 9.3 %reshape.70 = f32[16384,128]{1,0:T(8,128)} reshape(f32[64,32768]{1,0:T(8,128)} %pad_maximum_fusion) | data formatting | bytes 16777216 | tf_op jit(solution)/shard_map/reshape | solution.py:20
  49.6 0.0 copy-start.4
  49.6 0.0 copy-start.5
  49.6 0.0 copy-start.6
  49.6 0.0 copy-start.7
  49.6 0.0 copy-start.8
  49.6 0.0 copy-start.9
  49.6 0.0 reduce-scatter.2.cloned.1.call-update
  49.7 0.0 copy-start
  49.7 0.0 copy-start.1
  49.7 0.0 copy-start.2
  49.7 0.0 copy-start.3
  49.7 0.6 copy-done.4
  50.3 0.0 copy-done.5
  50.3 1.1 broadcast_in_dim.2
  51.4 13.1 %all-to-all-start = ((f32[64,1,2048]{2,1,0:T(1,128)}), f32[64,1,2048]{2,1,0:T(1,128)S(1)}, u32[]{:S(2)}, u32[]{:S(2)}) async-start(f32[64,1,2048]{2,1,0:T(1,128)} %broadcast_in_dim.2), calls=%async_computation.1 | async-start | bytes 1048576 | tf_op jit(solution)/shard_map/all_to_all | solution.py:31
  64.5 0.0 all-gather.2.cloned.1.call-start
  64.6 17.6 %all-to-all-done = f32[64,1,2048]{2,1,0:T(1,128)S(1)} async-done(((f32[64,1,2048]{2,1,0:T(1,128)}), f32[64,1,2048]{2,1,0:T(1,128)S(1)}, u32[]{:S(2)}, u32[]{:S(2)}) %all-to-all-start) | async-done | bytes 524320 | tf_op jit(solution)/shard_map/all_to_all | solution.py:31
  82.2 0.3 reduce_sum.9
  82.5 0.0 copy-done.6
  82.5 0.0 copy-done.7
  82.6 0.0 copy-done.8
  82.6 0.0 copy-done.9
  82.6 0.6 convert_bitcast_fusion.1
  83.2 0.1 copy.62
  83.3 0.1 copy.63
  83.4 117.8 %reduce-scatter.2.cloned.1.call-done = f32[256,128]{1,0:T(8,128)} async-done(((f32[16384,128]{1,0:T(8,128)}), f32[256,128]{1,0:T(8,128)}) %reduce-scatter.2.cloned.1.call-update) | async-done | bytes 131088 | tf_op jit(solution)/shard_map/reduce_scatter | solution.py:21
  201.2 0.9 multiply_multiply_fusion
  202.1 0.2 mul.127
  202.3 0.2 copy.60
  202.5 0.2 mul.133
  202.7 0.2 copy.59
  202.8 0.0 copy-done
  202.8 0.0 copy-done.1
  202.8 0.7 fusion
  203.5 0.0 copy-done.2
  203.5 0.0 copy-done.3
  203.5 0.7 convert_bitcast_fusion
  204.2 0.7 concatenate.11
  204.9 0.0 all-gather.2.cloned.1.call-update
  204.9 82.8 %all-gather.2.cloned.1.call-done = bf16[1024,2050]{1,0:T(8,128)(2,1)} async-done(((bf16[16,2050]{1,0:T(8,128)(2,1)}), bf16[1024,2050]{1,0:T(8,128)(2,1)}) %all-gather.2.cloned.1.call-update) | async-done | bytes 4198416 | tf_op jit(solution)/shard_map/all_gather | solution.py:52
  287.7 4.0 %slice_bitcast_fusion = (bf16[1024,1024]{0,1:T(8,128)(2,1)S(1)}, bf16[1024,1024]{1,0:T(8,128)(2,1)}) fusion(bf16[1024,2050]{1,0:T(8,128)(2,1)} %all-gather.2.cloned.1.call-done), kind=kLoop, calls=%fused_computation.1 | loop fusion | bytes 8388608 | tf_op jit(solution)/shard_map/transpose | solution.py:55
  291.7 2.5 copy.64
  294.2 2.0 slice_reduce_fusion
  (4 shorter events, 0.0 us)
Async XLA Ops:
  7.2 194.0 %reduce-scatter.2.cloned.1.call-start = ((), (), s32[]{:S(2)}) async-start(), calls=%async_computation.2 | async-start | bytes 8519680 | tf_op jit(solution)/shard_map/reduce_scatter | solution.py:21
  49.6 0.7 copy-start.4
  49.6 0.7 copy-start.5
  49.6 32.9 %copy-start.6 = (f32[16]{0:T(128)S(1)}, f32[16]{0:T(128)}, u32[]{:S(2)}) copy-start(f32[16]{0:T(128)} %param.19) | copy-start | bytes 196
  49.6 32.9 %copy-start.7 = (f32[16]{0:T(128)S(1)}, f32[16]{0:T(128)}, u32[]{:S(2)}) copy-start(f32[16]{0:T(128)} %param.23) | copy-start | bytes 196
  49.6 32.9 %copy-start.8 = (f32[16]{0:T(128)S(1)}, f32[16]{0:T(128)}, u32[]{:S(2)}) copy-start(f32[16]{0:T(128)} %param.18) | copy-start | bytes 196
  49.6 32.9 %copy-start.9 = (f32[16]{0:T(128)S(1)}, f32[16]{0:T(128)}, u32[]{:S(2)}) copy-start(f32[16]{0:T(128)} %param.22) | copy-start | bytes 196
  49.7 153.2 %copy-start = (f32[16,1024]{1,0:T(8,128)S(1)}, f32[16,1024]{1,0:T(8,128)}, u32[]{:S(2)}) copy-start(f32[16,1024]{1,0:T(8,128)} %param.16) | copy-start | bytes 196612
  49.7 153.2 %copy-start.1 = (f32[16,1024]{1,0:T(8,128)S(1)}, f32[16,1024]{1,0:T(8,128)}, u32[]{:S(2)}) copy-start(f32[16,1024]{1,0:T(8,128)} %param.20) | copy-start | bytes 196612
  49.7 153.8 %copy-start.2 = (f32[1024,16]{0,1:T(8,128)S(1)}, f32[1024,16]{0,1:T(8,128)}, u32[]{:S(2)}) copy-start(f32[1024,16]{0,1:T(8,128)} %param.17) | copy-start | bytes 196612
  49.7 153.8 %copy-start.3 = (f32[1024,16]{0,1:T(8,128)S(1)}, f32[1024,16]{0,1:T(8,128)}, u32[]{:S(2)}) copy-start(f32[1024,16]{0,1:T(8,128)} %param.21) | copy-start | bytes 196612
  51.4 30.8 %all-to-all-start = ((f32[64,1,2048]{2,1,0:T(1,128)}), f32[64,1,2048]{2,1,0:T(1,128)S(1)}, u32[]{:S(2)}, u32[]{:S(2)}) async-start(f32[64,1,2048]{2,1,0:T(1,128)} %broadcast_in_dim.2), calls=%async_computation.1 | async-start | bytes 1048576 | tf_op jit(solution)/shard_map/all_to_all | solution.py:31
  64.5 223.2 %all-gather.2.cloned.1.call-start = ((), (), s32[]{:S(2)}) async-start(), calls=%async_computation.3 | async-start | bytes 4526080 | tf_op jit(solution)/shard_map/all_gather | solution.py:52
Sparse Core Ops, SparseCore 0:
  49.8 151.3 reduce-scatter.1
  205.1 82.5 all-gather.1
where the time goes:
time: 304 us; the launch traced here: 303 us
  waiting for transfers between devices  218 us (72%)
  local copies, waits for them, and re-layouts  46.9 us (15%)
  between operations  14.2 us (5%)
  starting transfers between devices  13.2 us (4%)
  other arithmetic  10.5 us (3%)
    reduce_scatter x1, waiting for transfers between devices, sum_packed(): lax.psum_scatter(lines, axis, tiled=True).reshape(-1)  118 us
    all_gather x1, waiting for transfers between devices, gather_turned(): out, at, done = (lax.all_gather(both, axis, axis=0, tiled=True), 0, [])  82.8 us
    all_to_all x1, waiting for transfers between devices, from_everyone(): lax.all_to_all(jnp.broadcast_to(shard[None], (size, *shard.shape)), axis,...  17.6 us
    all_to_all x1, starting transfers between devices, from_everyone(): lax.all_to_all(jnp.broadcast_to(shard[None], (size, *shard.shape)), axis,...  13.1 us
    reshape x1, local copies, waits for them, and re-layouts, sum_packed(): jnp.pad(lines, ((0, 0), (0, width * 128 - lines.shape[1]))).reshape(-1, 128)  9.25 us
    transpose x1, local copies, waits for them, and re-layouts, in_blocks(): return jnp.moveaxis(shard.reshape(*before, size, -1, *after), dim, 0)  8.7 us
    unnamed x22, local copies, waits for them, and re-layouts  8.56 us
    concatenate x1, other arithmetic, sum_packed(): lines = jnp.concatenate([b.reshape(size, -1) for b in tiles], axis=1)  7.3 us
  transfers between devices with their start and end apart: 3, of which 3 were waited for; matrix products, arithmetic and copies ran while one was open for 1% of the time, Pallas kernels for 0%

commit v1 on v0

--- a/solution.py
+++ b/solution.py
@@ -5,6 +5,11 @@
 
 learn_rate = 0.05
 hold_rate = 0.9
+
+
+def swapped_in(x, mesh_axis, d):
+    sent = jnp.stack([x] * lax.axis_size(mesh_axis))
+    return jnp.concatenate(lax.all_to_all(sent, mesh_axis, 0, 0), axis=d)
 
 
 def in_blocks(shard, dim, size):
@@ -49,7 +54,7 @@
 def gather_turned(arrays, axis, dims):
     turned = [jnp.moveaxis(a, dim, 0) for a, dim in zip(arrays, dims)]
     both = jnp.concatenate([t.reshape(len(t), -1) for t in turned], axis=1)
-    out, at, done = (lax.all_gather(both, axis, axis=0, tiled=True), 0, [])
+    out, at, done = (swapped_in(both, axis, 0), 0, [])
     for t, dim in zip(turned, dims):
         section = out[:, at : at + t[0].size].reshape(-1, *t.shape[1:])
         done.append(jnp.moveaxis(section, 0, dim))

time: 304 us -> 333 us (1.095)
  blocking collectives: 0 us -> 115 us
  waiting for transfers between devices: 218 us -> 136 us
  local copies, waits for them, and re-layouts: 46.9 us -> 43.5 us
    all_to_all x0 -> x1, blocking collectives: none -> 115 us  [swapped_in(): return jnp.concatenate(lax.all_to_all(sent, mesh_axis, 0, 0), axis=d)]
    all_gather x1 -> x0, waiting for transfers between devices: 82.8 us -> none  [gather_turned(): out, at, done = (lax.all_gather(both, axis, axis=0, tiled=True), 0, [])]
  transfers between devices with their start and end apart: 3 -> 2, of which waited for: 3 -> 2; matrix products, arithmetic and copies ran while one was open for 1% -> 1% of each run, Pallas kernels for 0% -> 0%
where the time goes in v1:
time: 333 us; the launch traced here: 332 us
  waiting for transfers between devices  136 us (41%)
  blocking collectives  115 us (35%)
  local copies, waits for them, and re-layouts  43.5 us (13%)
  between operations  14.2 us (4%)
  starting transfers between devices  13.2 us (4%)
  other arithmetic  10.5 us (3%)
    reduce_scatter x1, waiting for transfers between devices, sum_packed(): lax.psum_scatter(lines, axis, tiled=True).reshape(-1)  118 us
    all_to_all x1, blocking collectives, swapped_in(): return jnp.concatenate(lax.all_to_all(sent, mesh_axis, 0, 0), axis=d)  115 us
    all_to_all x1, waiting for transfers between devices, from_everyone(): lax.all_to_all(jnp.broadcast_to(shard[None], (size, *shard.shape)), axis,...  17.7 us
    all_to_all x1, starting transfers between devices, from_everyone(): lax.all_to_all(jnp.broadcast_to(shard[None], (size, *shard.shape)), axis,...  13.1 us
    reshape x1, local copies, waits for them, and re-layouts, sum_packed(): jnp.pad(lines, ((0, 0), (0, width * 128 - lines.shape[1]))).reshape(-1, 128)  9.25 us
    transpose x1, local copies, waits for them, and re-layouts, in_blocks(): return jnp.moveaxis(shard.reshape(*before, size, -1, *after), dim, 0)  8.7 us
    unnamed x22, local copies, waits for them, and re-layouts  8.56 us
    concatenate x1, other arithmetic, sum_packed(): lines = jnp.concatenate([b.reshape(size, -1) for b in tiles], axis=1)  7.29 us
  transfers between devices with their start and end apart: 2, of which 2 were waited for; matrix products, arithmetic and copies ran while one was open for 1% of the time, Pallas kernels for 0%

profile of v1, /device:TPU:1, one launch (start us, length us, event | category | flops | bytes accessed | tf_op | source)
XLA Modules:
  0.0 332.2 jit_solution(8138375754436686522)
XLA Ops:
  7.2 0.0 reduce-scatter.2.cloned.1.call-start
  7.2 5.4 %copy.58 = f32[1,1024,1024]{1,2,0:T(8,128)} copy(f32[1,1024,1024]{2,1,0:T(8,128)} %param.13) | data formatting | bytes 8388608 | tf_op args[1]
  12.6 8.7 %copy.59 = f32[64,1024,16]{0,2,1:T(8,128)} copy(f32[64,1024,16]{1,2,0:T(8,128)} %bitcast.18) | data formatting | bytes 8388608 | tf_op jit(solution)/shard_map/transpose | solution.py:17
  21.3 6.8 %copy.60 = f32[64,16384]{1,0:T(8,128)} copy(f32[64,16384]{0,1:T(8,128)} %bitcast.15) | data formatting | bytes 8388608 | tf_op jit(solution)/shard_map/reshape | solution.py:23
  28.1 4.9 %reshape_reshape_squeeze.3 = f32[64,16384]{1,0:T(8,128)} reshape(f32[1,1024,1024]{2,1,0:T(8,128)} %param.12) | data formatting | bytes 8388608 | tf_op jit(solution)/shard_map/reshape;reshape;squeeze | solution.py:23
  33.1 7.3 %pad_maximum_fusion = f32[64,32768]{1,0:T(8,128)} fusion(f32[64,16384]{1,0:T(8,128)} %copy.60, f32[64,16384]{1,0:T(8,128)} %reshape_reshape_squeeze.3), kind=kLoop, calls=%fused_computation | loop fusion | flops 2097152 | bytes 16777216 | tf_op jit(solution)/shard_map/concatenate | solution.py:23
  40.4 9.3 %reshape.75 = f32[16384,128]{1,0:T(8,128)} reshape(f32[64,32768]{1,0:T(8,128)} %pad_maximum_fusion) | data formatting | bytes 16777216 | tf_op jit(solution)/shard_map/reshape | solution.py:25
  49.6 0.0 copy-start.4
  49.6 0.0 copy-start.5
  49.6 0.0 copy-start.6
  49.6 0.0 copy-start.7
  49.6 0.0 copy-start.8
  49.6 0.0 copy-start.9
  49.6 0.0 reduce-scatter.2.cloned.1.call-update
  49.7 0.0 copy-start
  49.7 0.0 copy-start.1
  49.7 0.0 copy-start.2
  49.7 0.0 copy-start.3
  49.7 0.6 copy-done.4
  50.3 0.0 copy-done.5
  50.3 1.1 broadcast_in_dim.2
  51.4 13.1 %all-to-all-start = ((f32[64,1,2048]{2,1,0:T(1,128)}), f32[64,1,2048]{2,1,0:T(1,128)S(1)}, u32[]{:S(2)}, u32[]{:S(2)}) async-start(f32[64,1,2048]{2,1,0:T(1,128)} %broadcast_in_dim.2), calls=%async_computation.1 | async-start | bytes 1048576 | tf_op jit(solution)/shard_map/all_to_all | solution.py:36
  64.5 17.7 %all-to-all-done = f32[64,1,2048]{2,1,0:T(1,128)S(1)} async-done(((f32[64,1,2048]{2,1,0:T(1,128)}), f32[64,1,2048]{2,1,0:T(1,128)S(1)}, u32[]{:S(2)}, u32[]{:S(2)}) %all-to-all-start) | async-done | bytes 524320 | tf_op jit(solution)/shard_map/all_to_all | solution.py:36
  82.2 0.3 reduce_sum.9
  82.5 0.0 copy-done.6
  82.6 0.0 copy-done.7
  82.6 0.0 copy-done.8
  82.6 0.0 copy-done.9
  82.6 0.6 convert_bitcast_fusion.1
  83.2 0.1 copy.64
  83.3 0.1 copy.65
  83.4 117.8 %reduce-scatter.2.cloned.1.call-done = f32[256,128]{1,0:T(8,128)} async-done(((f32[16384,128]{1,0:T(8,128)}), f32[256,128]{1,0:T(8,128)}) %reduce-scatter.2.cloned.1.call-update) | async-done | bytes 131088 | tf_op jit(solution)/shard_map/reduce_scatter | solution.py:26
  201.2 0.9 multiply_multiply_fusion
  202.1 0.2 mul.127
  202.3 0.2 copy.62
  202.5 0.2 mul.133
  202.7 0.2 copy.61
  202.9 0.0 copy-done
  202.9 0.0 copy-done.1
  202.9 0.7 fusion
  203.5 0.0 copy-done.2
  203.5 0.0 copy-done.3
  203.5 0.7 convert_bitcast_fusion
  204.2 0.1 concatenate.11
  204.3 0.3 stack.2
  204.6 115.4 %all_to_all.11 = bf16[64,16,2050]{2,1,0:T(8,128)(2,1)S(1)} all-to-all(bf16[64,16,2050]{2,1,0:T(8,128)(2,1)S(1)} %stack.2), channel_id=1, replica_groups=mesh['replica'=64,'model'=4] {'replica'}, dimensions={0} | all-to-all | bytes 8396800 | tf_op jit(solution)/shard_map/all_to_all | solution.py:12
  320.0 1.9 slice_bitcast_fusion
  321.9 0.9 slice_reduce_fusion
  322.8 2.5 copy.66
  (4 shorter events, 0.0 us)
Async XLA Ops:
  7.2 194.0 %reduce-scatter.2.cloned.1.call-start = ((), (), s32[]{:S(2)}) async-start(), calls=%async_computation.3 | async-start | bytes 8519680 | tf_op jit(solution)/shard_map/reduce_scatter | solution.py:26
  49.6 0.7 copy-start.4
  49.6 0.7 copy-start.5
  49.6 32.9 %copy-start.6 = (f32[16]{0:T(128)S(1)}, f32[16]{0:T(128)}, u32[]{:S(2)}) copy-start(f32[16]{0:T(128)} %param.19) | copy-start | bytes 196
  49.6 32.9 %copy-start.7 = (f32[16]{0:T(128)S(1)}, f32[16]{0:T(128)}, u32[]{:S(2)}) copy-start(f32[16]{0:T(128)} %param.23) | copy-start | bytes 196
  49.6 32.9 %copy-start.8 = (f32[16]{0:T(128)S(1)}, f32[16]{0:T(128)}, u32[]{:S(2)}) copy-start(f32[16]{0:T(128)} %param.18) | copy-start | bytes 196
  49.6 32.9 %copy-start.9 = (f32[16]{0:T(128)S(1)}, f32[16]{0:T(128)}, u32[]{:S(2)}) copy-start(f32[16]{0:T(128)} %param.22) | copy-start | bytes 196
  49.7 153.2 %copy-start = (f32[16,1024]{1,0:T(8,128)S(1)}, f32[16,1024]{1,0:T(8,128)}, u32[]{:S(2)}) copy-start(f32[16,1024]{1,0:T(8,128)} %param.16) | copy-start | bytes 196612
  49.7 153.2 %copy-start.1 = (f32[16,1024]{1,0:T(8,128)S(1)}, f32[16,1024]{1,0:T(8,128)}, u32[]{:S(2)}) copy-start(f32[16,1024]{1,0:T(8,128)} %param.20) | copy-start | bytes 196612
  49.7 153.8 %copy-start.2 = (f32[1024,16]{0,1:T(8,128)S(1)}, f32[1024,16]{0,1:T(8,128)}, u32[]{:S(2)}) copy-start(f32[1024,16]{0,1:T(8,128)} %param.17) | copy-start | bytes 196612
  49.7 153.8 %copy-start.3 = (f32[1024,16]{0,1:T(8,128)S(1)}, f32[1024,16]{0,1:T(8,128)}, u32[]{:S(2)}) copy-start(f32[1024,16]{0,1:T(8,128)} %param.21) | copy-start | bytes 196612
  51.4 30.8 %all-to-all-start = ((f32[64,1,2048]{2,1,0:T(1,128)}), f32[64,1,2048]{2,1,0:T(1,128)S(1)}, u32[]{:S(2)}, u32[]{:S(2)}) async-start(f32[64,1,2048]{2,1,0:T(1,128)} %broadcast_in_dim.2), calls=%async_computation.1 | async-start | bytes 1048576 | tf_op jit(solution)/shard_map/all_to_all | solution.py:36
Sparse Core Ops, SparseCore 0:
  49.8 151.3 reduce-scatter.1
